TPU v7x, 32 devices: a whole 2x2x4 slice. The times are simulated.
32 devices in a mesh: rows: 8 (over y, x, core), dim: 4 (over z).
Axes of the slice: x: 2, y: 2, z: 4, core: 2. Of those that a mesh axis runs over, the one named last changes fastest.
Arguments:
- entity_table: float32 [131072, 512], P(('rows', 'dim')), may hold values from -2.5 to 2.5
- relations: float32 [822, 512], replicated, may hold values from -6 to 6
- thresholds: float32 [64], replicated, may hold values from 0.2 to 2
- head_ids: int32 [2048], replicated, may hold values from 0 to 131071
- rel_ids: int32 [2048], replicated, may hold values from 0 to 821
- thr_idx: int32 [2048], replicated, may hold values from 0 to 63
Outputs:
- serving_table: float32 [131072, 512], P('rows', 'dim')
- fraction: float32 [2048], P(('rows', 'dim'))
All inputs are finite; a program needn't handle non-finite values.
Results may differ from a plain program's by a relative error of at most 0.0011.
Values sent between devices are 32-bit elements; how exact they have to be, the bound alone decides.
A program may use at most 128 MiB of HBM per device.

v0:
```python
import jax
import jax.numpy as jnp
from jax import lax
from jax.sharding import PartitionSpec as P

sharpness = 2.0


def pick_rows(table, head_ids, start):
    count = table.shape[0]
    local = head_ids - start
    owned = (local >= 0) & (local < count)
    picked = jnp.take(table, jnp.clip(local, 0, count - 1), axis=0)
    return jnp.where(owned[:, None], picked, jnp.zeros_like(picked))


def shards(entity_table, relations, thresholds, head_ids, rel_ids, thr_idx):
    local_rows = entity_table.shape[0]
    width = entity_table.shape[1]
    total_ents = local_rows * lax.axis_size("rows") * lax.axis_size("dim")
    serving = lax.all_to_all(entity_table, "dim", split_axis=1, concat_axis=0, tiled=True)
    start = (lax.axis_index("rows") * lax.axis_size("dim") + lax.axis_index("dim")) * local_rows
    partial_value = pick_rows(entity_table, head_ids, start)
    head_vecs = lax.psum(partial_value, ("rows", "dim"))
    query = (head_vecs * jnp.take(relations, rel_ids, axis=0)).astype(jnp.bfloat16)
    ent_low = entity_table.astype(jnp.bfloat16)
    level = jnp.take(thresholds, thr_idx)
    queries = query.shape[0]
    query_blocks = query.reshape(queries // 512, 512, width)
    level_blocks = level.reshape(queries // 512, 512)

    def score_block(pair):
        rows_q, rows_level = pair
        score = jnp.dot(rows_q, ent_low.T, preferred_element_type=jnp.float32)
        soft = jax.nn.sigmoid(sharpness * (score - rows_level[:, None]))
        return jnp.sum(soft, axis=1) * (1.0 / total_ents)

    partial_share = lax.map(score_block, (query_blocks, level_blocks)).reshape(queries)
    fraction = lax.psum_scatter(partial_share, ("rows", "dim"), scatter_dimension=0, tiled=True)
    return (serving, fraction)


def solution(mesh):
    placed = (P(("rows", "dim"), None), P(), P(), P(), P(), P())
    return jax.shard_map(
        shards,
        mesh=mesh,
        in_specs=placed,
        out_specs=(P("rows", "dim"), P(("rows", "dim"))),
        check_vma=False,
    )
```

profile of v0, /device:TPU:0, one launch (start us, length us, event | category | flops | bytes accessed | tf_op | source)
XLA Modules:
  0.0 399.6 jit_solution(839341070260288952)
XLA Ops:
  7.2 0.0 copy-start
  7.2 7.4 %copy_bitcast_fusion = f32[4096,4,128]{2,0,1:T(8,128)} fusion(f32[4096,512]{1,0:T(8,128)} %param.8), kind=kLoop, calls=%fused_computation.9 | loop fusion | bytes 16777216 | tf_op jit(solution)/shard_map/all_to_all | solution.py:21
  14.6 6.5 %all-to-all-start = ((f32[4096,4,128]{2,0,1:T(8,128)}), f32[4096,4,128]{2,0,1:T(8,128)}, u32[]{:S(2)}, u32[]{:S(2)}) async-start(f32[4096,4,128]{2,0,1:T(8,128)} %copy_bitcast_fusion), calls=%async_computation | async-start | bytes 16777216 | tf_op jit(solution)/shard_map/all_to_all | solution.py:21
  21.1 12.9 %gather_fusion = f32[2048,512]{1,0:T(8,128)} fusion(f32[4096,512]{1,0:T(8,128)} %param.8, s32[2048]{0:T(1024)S(1)} %fusion.5), kind=kCustom, calls=%fused_computation | custom fusion | bytes 8396800 | tf_op jit(solution)/shard_map/jit(_take)/gather | solution.py:13
  34.1 3.9 select_select_fusion
  38.0 0.0 all-reduce.3.cloned.1.call-update
  38.0 0.0 copy-start.1
  38.0 0.0 copy-start.4
  38.1 0.0 copy-start.2
  38.1 5.9 %convert_element_type.7 = bf16[4096,512]{1,0:T(8,128)(2,1)} convert(f32[4096,512]{1,0:T(8,128)} %param.8) | non-fusion elementwise | flops 2097152 | bytes 12582912 | tf_op jit(solution)/shard_map/convert_element_type | solution.py:26
  44.0 0.7 fusion.9
  44.6 0.7 fusion.7
  45.4 0.7 fusion.6
  46.1 0.7 fusion.8
  46.8 39.9 %select_select_fusion.1 = f32[2048]{0:T(1024)S(1)} fusion(s32[2048]{0:T(1024)S(1)} %copy-done.4, f32[]{:T(128)} %bitcast.6, f32[]{:T(128)} %bitcast.7, f32[]{:T(128)} %bitcast.8, f32[]{:T(128)} %bitcast.9, f32[]{:T(128)} %bitcast.10, f32[]{:T(128)} %bitcast.11, f32[]{:T(128)} %bitcast.12, f32[]{:T(128)} %bitcast.13, f32[]{:T(128)} %bitcast.14, f32[]{:T(128)} %bitcast.15, ...), kind=kLoop, calls=%fused_computation.15 | loop fusion | flops 272384 | bytes 16640 | tf_op jit(solution)/shard_map/jit(_take)/select_n | solution.py:27
  86.8 0.0 copy-done.2
  86.8 8.9 %gather_fusion.1 = f32[2048,512]{1,0:T(8,128)} fusion(f32[822,512]{1,0:T(8,128)S(1)} %copy-done, s32[2048]{0:T(1024)S(1)} %fusion.4), kind=kCustom, calls=%fused_computation.1 | custom fusion | bytes 8396800 | tf_op jit(solution)/shard_map/jit(_take)/gather | solution.py:25
  95.7 223.5 %all-reduce.3.cloned.1.call-done = f32[2048,512]{1,0:T(8,128)} async-done(((f32[2048,512]{1,0:T(8,128)}), f32[2048,512]{1,0:T(8,128)}) %all-reduce.3.cloned.1.call-update) | async-done | bytes 4194320 | tf_op jit(solution)/shard_map/psum | solution.py:24
  319.2 4.7 %multiply_convert_fusion = bf16[2048,512]{1,0:T(8,128)(2,1)} fusion(f32[2048,512]{1,0:T(8,128)} %all-reduce.3.cloned.1.call-done, f32[2048,512]{1,0:T(8,128)} %gather_fusion.1, pred[2048]{0:T(1024)(128)(4,1)S(1)} %compare_and_fusion), kind=kLoop, calls=%fused_computation.10 | loop fusion | flops 3145728 | bytes 10487808 | tf_op jit(solution)/shard_map/convert_element_type | solution.py:25
  323.9 22.9 %while.10 = (s32[]{:T(128)}, f32[4,512]{1,0:T(4,128)S(1)}, bf16[4,512,512]{2,1,0:T(8,128)(2,1)}, bf16[4096,512]{1,0:T(8,128)(2,1)}, f32[4,512]{1,0:T(4,128)S(1)}, /*index=5*/s32[]{:T(128)}, s32[]{:T(128)}) while((s32[]{:T(128)}, f32[4,512]{1,0:T(4,128)S(1)}, bf16[4,512,512]{2,1,0:T(8,128)(2,1)}, bf16[4096,512]{1,0:T(8,128)(2,1)}, ...), condition=%wide.region_3.4_spmd, body=%wide.region_1.3_spmd.sunk | while | flops 2160066560 | bytes 4735073 | solution.py:38
  323.9 5.6 %fusion.17 = f32[512]{0:T(512)S(1)} fusion(bf16[4096,512]{1,0:T(8,128)(2,1)} %get-tuple-element.154, f32[512]{0:T(512)S(1)} %bitcast.91, bf16[4,512,512]{2,1,0:T(8,128)(2,1)} %get-tuple-element.153, s32[]{:T(128)S(6)} %copy.17), kind=kOutput, calls=%fused_computation.3.clone.1 | convolution fusion | flops 2160066048 | bytes 4722692 | tf_op jit(solution)/shard_map/while/body/eval_jaxpr/dot_general | solution.py:34
  329.6 0.1 dynamic_update_slice.5
  329.6 5.6 %fusion.17 = f32[512]{0:T(512)S(1)} fusion(bf16[4096,512]{1,0:T(8,128)(2,1)} %get-tuple-element.154, f32[512]{0:T(512)S(1)} %bitcast.91, bf16[4,512,512]{2,1,0:T(8,128)(2,1)} %get-tuple-element.153, s32[]{:T(128)S(6)} %copy.17), kind=kOutput, calls=%fused_computation.3.clone.1 | convolution fusion | flops 2160066048 | bytes 4722692 | tf_op jit(solution)/shard_map/while/body/eval_jaxpr/dot_general | solution.py:34
  335.3 0.1 dynamic_update_slice.5
  335.4 5.6 %fusion.17 = f32[512]{0:T(512)S(1)} fusion(bf16[4096,512]{1,0:T(8,128)(2,1)} %get-tuple-element.154, f32[512]{0:T(512)S(1)} %bitcast.91, bf16[4,512,512]{2,1,0:T(8,128)(2,1)} %get-tuple-element.153, s32[]{:T(128)S(6)} %copy.17), kind=kOutput, calls=%fused_computation.3.clone.1 | convolution fusion | flops 2160066048 | bytes 4722692 | tf_op jit(solution)/shard_map/while/body/eval_jaxpr/dot_general | solution.py:34
  341.0 0.1 dynamic_update_slice.5
  341.1 5.6 %fusion.17 = f32[512]{0:T(512)S(1)} fusion(bf16[4096,512]{1,0:T(8,128)(2,1)} %get-tuple-element.154, f32[512]{0:T(512)S(1)} %bitcast.91, bf16[4,512,512]{2,1,0:T(8,128)(2,1)} %get-tuple-element.153, s32[]{:T(128)S(6)} %copy.17), kind=kOutput, calls=%fused_computation.3.clone.1 | convolution fusion | flops 2160066048 | bytes 4722692 | tf_op jit(solution)/shard_map/while/body/eval_jaxpr/dot_general | solution.py:34
  346.8 0.1 dynamic_update_slice.5
  346.8 39.4 %all-reduce = f32[2048]{0:T(1024)S(1)} all-reduce(f32[2048]{0:T(1024)S(1)} %bitcast.92), channel_id=2, replica_groups=mesh['rows'=8,'dim'=4] {'rows','dim'}, use_global_device_ids=true, to_apply=%region_4.5.clone | all-reduce | flops 2048 | bytes 16384
  386.3 0.6 dynamic-slice
  386.9 0.0 all-to-all-done
  386.9 5.9 %copy.22 = f32[16384,128]{1,0:T(8,128)} copy(f32[16384,128]{1,0:T(8,128)} %bitcast.4) | data formatting | bytes 16777216
  (21 shorter events, 0.1 us)
Async XLA Ops:
  7.2 79.7 %copy-start = (f32[822,512]{1,0:T(8,128)S(1)}, f32[822,512]{1,0:T(8,128)}, u32[]{:S(2)}) copy-start(f32[822,512]{1,0:T(8,128)} %param.9) | copy-start | bytes 5050372
  14.6 6.5 %copy-start.3 = (s32[2048]{0:T(1024)S(1)}, s32[2048]{0:T(1024)}, u32[]{:S(2)}) copy-start(s32[2048]{0:T(1024)} %param.11) | copy-start | bytes 24580
  14.6 372.2 %all-to-all-start = ((f32[4096,4,128]{2,0,1:T(8,128)}), f32[4096,4,128]{2,0,1:T(8,128)}, u32[]{:S(2)}, u32[]{:S(2)}) async-start(f32[4096,4,128]{2,0,1:T(8,128)} %copy_bitcast_fusion), calls=%async_computation | async-start | bytes 16777216 | tf_op jit(solution)/shard_map/all_to_all | solution.py:21
  21.1 298.1 %all-reduce.3.cloned.1.call-start = ((), (), s32[]{:S(2)}) async-start(), calls=%async_computation.1 | async-start | bytes 8388608 | tf_op jit(solution)/shard_map/psum | solution.py:24
  38.0 5.9 %copy-start.1 = (f32[64]{0:T(128)S(1)}, f32[64]{0:T(128)}, u32[]{:S(2)}) copy-start(f32[64]{0:T(128)} %param.10) | copy-start | bytes 772
  38.0 8.8 %copy-start.4 = (s32[2048]{0:T(1024)S(1)}, s32[2048]{0:T(1024)}, u32[]{:S(2)}) copy-start(s32[2048]{0:T(1024)} %param.13) | copy-start | bytes 24580
  38.1 48.7 %copy-start.2 = (s32[2048]{0:T(1024)S(1)}, s32[2048]{0:T(1024)}, u32[]{:S(2)}) copy-start(s32[2048]{0:T(1024)} %param.12) | copy-start | bytes 24580
Sparse Core Ops, SparseCore 0:
  38.1 280.9 all-reduce.2
where the time goes:
time: 401 us; the launch traced here: 400 us
  waiting for transfers between devices  223 us (56%)
  other arithmetic  54.6 us (14%)
  blocking collectives  39.4 us (10%)
  local copies, waits for them, and re-layouts  38.8 us (10%)
  matrix products  22.6 us (6%)
  between operations  14.2 us (4%)
  starting transfers between devices  6.48 us (2%)
    psum x1, waiting for transfers between devices, shards(): head_vecs = lax.psum(partial_value, ('rows', 'dim'))  223 us
    select_n x1, other arithmetic, shards(): level = jnp.take(thresholds, thr_idx)  39.9 us
    unnamed x1, blocking collectives  39.4 us
    dot_general x4, matrix products, score_block(): score = jnp.dot(rows_q, ent_low.T, preferred_element_type=jnp.float32)  22.6 us
    gather x1, local copies, waits for them, and re-layouts, pick_rows(): picked = jnp.take(table, jnp.clip(local, 0, count - 1), axis=0)  12.9 us
    gather x1, local copies, waits for them, and re-layouts, shards(): jnp.take(relations, rel_ids, axis=0)  8.85 us
  transfers between devices with their start and end apart: 2, of which 1 were waited for; matrix products, arithmetic and copies ran while one was open for 26% of the time, Pallas kernels for 0%

commit v1 on v0

v1 whole, which is shorter than its diff:
```python
import functools
import jax
import jax.numpy as jnp
from jax import lax
from jax.sharding import PartitionSpec as P
from jax.experimental import pallas as pl
from jax.experimental.pallas import tpu as pltpu

MESH = pl.DeviceIdType.MESH
sharpness = 2.0
lanes = 128
units = 16


def plan_for(size):
    middles = 2 * bits_of(size) - 1
    entry = 4
    middle = min(2, (units - entry - 1) // middles)
    return (entry,) + (middle,) * middles + (units - entry - middle * middles,)


def bits_of(size):
    assert size & (size - 1) == 0
    return size.bit_length() - 1


def kernel(
    R, N, total_ents, head_ids, rel_ids, thr, thr_idx, rel, table, *others
):
    slabs = others[:-23]
    (
        serving, frac_out,
        tab, low, part, recv, full, qb, lev, frac, fr_rows, fr_dim, fr_sum,
        load_sem, own_sem, a2a_send, a2a_recv, ex_send, ex_recv, f_send, f_recv, g_send, g_recv,
    ) = others[-23:]
    r = lax.axis_index("rows")
    d = lax.axis_index("dim")
    n, width = table.shape
    slab = width // N
    Q = part.shape[0]
    half_q = Q // 2
    chunk = n // units
    plan = plan_for(N)

    load = pltpu.make_async_copy(table, tab, load_sem)
    load.start()

    row_peers = [lax.rem(r + k, R) for k in range(1, R)]
    dim_peers = [lax.rem(d + k, N) for k in range(1, N)]
    barrier = pltpu.get_barrier_semaphore()
    for t in row_peers:
        pl.semaphore_signal(barrier, inc=1, device_id=(t, d), device_id_type=MESH)
    for t in dim_peers:
        pl.semaphore_signal(barrier, inc=1, device_id=(r, t), device_id_type=MESH)
    pl.semaphore_wait(barrier, R + N - 2)

    def slab_rows(source, t, start, rows):
        if slabs:
            return slabs[0].at[t, pl.ds(start, rows), :]
        return source.at[pl.ds(start, rows), pl.ds(pl.multiple_of(t * slab, slab), slab)]

    a2a = []
    starts = [sum(plan[:i]) * chunk for i in range(len(plan))]

    def issue(piece):
        rows = plan[piece] * chunk
        for k, t in enumerate(dim_peers):
            copy = pltpu.make_async_remote_copy(
                src_ref=slab_rows(table, t, starts[piece], rows),
                dst_ref=serving.at[pl.ds(pl.multiple_of(d * n + starts[piece], 8), rows), :],
                send_sem=a2a_send.at[piece, k],
                recv_sem=a2a_recv.at[piece, k],
                device_id=(r, t),
                device_id_type=MESH,
            )
            copy.start()
            a2a.append(copy)

    issue(0)

    load.wait()
    own = pltpu.make_async_copy(
        slab_rows(tab, d, 0, n),
        serving.at[pl.ds(pl.multiple_of(d * n, 8), n), :],
        own_sem,
    )
    own.start()
    first = (r * N + d) * n

    def pick(i, carry):
        base = pl.multiple_of(i * 8, 8)
        rows = []
        for j in range(8):
            local = head_ids[base + j] - first
            owned = jnp.logical_and(local >= 0, local < n)
            row = tab[pl.ds(jnp.clip(local, 0, n - 1), 1), :]
            rows.append(jnp.where(owned, row, jnp.zeros_like(row)))
        part[pl.ds(base, 8), :] = jnp.concatenate(rows, axis=0)
        return carry

    lax.fori_loop(0, Q // 8, pick, 0)

    row_bits = [("rows", b) for b in range(bits_of(R))]
    dim_bits = [("dim", b) for b in range(bits_of(N))]
    orders = [row_bits + dim_bits, row_bits[:1] + row_bits[:0:-1] + dim_bits]
    steps = len(orders[0])
    nrow = len(row_bits)

    def bit_and_peer(axis, b):
        me = r if axis == "rows" else d
        bit = lax.rem(me // (2 ** b), 2)
        other = me + (1 - 2 * bit) * (2 ** b)
        return bit, ((other, d) if axis == "rows" else (r, other))

    def exchange(src, dst, peer, stream, slot):
        copy = pltpu.make_async_remote_copy(
            src_ref=src, dst_ref=dst,
            send_sem=ex_send.at[stream, slot], recv_sem=ex_recv.at[stream, slot],
            device_id=peer, device_id_type=MESH,
        )
        copy.start()
        return copy

    offset = [0, half_q]
    size = half_q
    into = 0
    piece = 1
    for k in range(steps):
        h = size // 2
        copies = []
        for s in range(2):
            bit, peer = bit_and_peer(*orders[s][k])
            gone = pl.multiple_of(offset[s] + (1 - bit) * h, 8)
            copies.append(exchange(
                part.at[pl.ds(gone, h), :],
                recv.at[pl.ds(s * half_q + into, h), :],
                peer, s, k,
            ))
            offset[s] = pl.multiple_of(offset[s] + bit * h, 8)
        if k >= nrow:
            if piece < len(plan) - 1:
                issue(piece)
                piece += 1
        if k == 0:
            def narrow(i, carry):
                at = pl.multiple_of(i * 128, 128)
                low[pl.ds(at, 128), :] = tab[pl.ds(at, 128), :].astype(jnp.bfloat16)
                return carry

            lax.fori_loop(0, n // 128, narrow, 0)
        if k == 1:
            idx = thr_idx[...]

            def choose(t, acc):
                return jnp.where(idx == t, thr[t], acc)

            lev[...] = lax.fori_loop(0, thr.shape[0], choose, jnp.zeros(idx.shape, jnp.float32))
        for s in range(2):
            copies[s].wait()
            if h >= 64:
                def add(i, carry, s=s, into=into):
                    at = pl.ds(pl.multiple_of(offset[s] + i * 64, 8), 64)
                    frm = pl.ds(s * half_q + into + i * 64, 64)
                    part[at, :] = part[at, :] + recv[frm, :]
                    return carry

                lax.fori_loop(0, h // 64, add, 0)
            else:
                at = pl.ds(offset[s], h)
                part[at, :] = part[at, :] + recv[pl.ds(s * half_q + into, h), :]
        into += h
        size = h

    for s in range(2):
        def form(i, carry, s=s):
            base = pl.multiple_of(offset[s] + i * 8, 8)
            rows = [rel[pl.ds(rel_ids[base + j], 1), :] for j in range(8)]
            full[pl.ds(base, 8), :] = part[pl.ds(base, 8), :] * jnp.concatenate(rows, axis=0)
            return carry

        lax.fori_loop(0, size // 8, form, 0)

    def count_pair(q0, q1):
        qb[:lanes, :] = full[pl.ds(q0, lanes), :].astype(jnp.bfloat16)
        qb[lanes:, :] = full[pl.ds(q1, lanes), :].astype(jnp.bfloat16)
        i0 = q0 // lanes
        i1 = q1 // lanes
        level = jnp.concatenate([lev[i0], lev[i1]], axis=1)
        rows = 512

        def tile(i, acc):
            at = pl.multiple_of(i * rows, rows)
            score = lax.dot_general(
                low[pl.ds(at, rows), :], qb[...], (((1,), (1,)), ((), ())),
                preferred_element_type=jnp.float32,
            )
            soft = jax.nn.sigmoid(sharpness * (score - level))
            return acc + jnp.sum(soft.reshape(rows // 8, 8, 2 * lanes), axis=0)

        acc = lax.fori_loop(0, n // rows, tile, jnp.zeros((8, 2 * lanes), jnp.float32))
        share = jnp.sum(acc, axis=0, keepdims=True) * (1.0 / total_ents)
        frac[i0] = share[:, :lanes]
        frac[i1] = share[:, lanes:]

    def count(starts_, rows):
        def body(i, carry):
            count_pair(pl.multiple_of(starts_[0] + i * lanes, lanes), pl.multiple_of(starts_[1] + i * lanes, lanes))
            return carry

        lax.fori_loop(0, rows // lanes, body, 0)

    pending = None
    counted = False
    slot = steps
    for k in reversed(range(steps)):
        copies = []
        there = []
        for s in range(2):
            bit, peer = bit_and_peer(*orders[s][k])
            here = full.at[pl.ds(offset[s], size), :]
            copies.append(exchange(here, here, peer, s, slot))
            there.append(pl.multiple_of(offset[s] + (1 - 2 * bit) * size, 8))
            offset[s] = pl.multiple_of(offset[s] - bit * size, 8)
        slot += 1
        if k >= nrow:
            issue(piece)
            piece += 1
        if pending is not None:
            count(*pending)
            pending = None
        for copy in copies:
            copy.wait()
        size = 2 * size
        if k <= nrow and size >= lanes:
            pending = (there, size // 2) if counted else (list(offset), size)
            counted = True
    count(*pending)

    per = frac.shape[0] // R
    sends = []
    for k, t in enumerate(row_peers):
        copy = pltpu.make_async_remote_copy(
            src_ref=frac.at[pl.ds(t * per, per)],
            dst_ref=fr_rows.at[R - 2 - k],
            send_sem=f_send.at[k], recv_sem=f_recv.at[R - 2 - k],
            device_id=(t, d), device_id_type=MESH,
        )
        copy.start()
        sends.append(copy)
    total = frac[pl.ds(r * per, per)]
    for k in range(R - 1):
        sends[k].wait_send()
        pltpu.make_async_remote_copy(
            src_ref=frac.at[pl.ds(r * per, per)],
            dst_ref=fr_rows.at[k], send_sem=f_send.at[k], recv_sem=f_recv.at[k],
            device_id=(row_peers[k], d), device_id_type=MESH,
        ).wait_recv()
        total = total + fr_rows[k]
    fr_sum[...] = total
    sends = []
    for k, t in enumerate(dim_peers):
        copy = pltpu.make_async_remote_copy(
            src_ref=fr_sum, dst_ref=fr_dim.at[N - 2 - k],
            send_sem=g_send.at[k], recv_sem=g_recv.at[N - 2 - k],
            device_id=(r, t), device_id_type=MESH,
        )
        copy.start()
        sends.append(copy)
    for k in range(N - 1):
        sends[k].wait_send()
        pltpu.make_async_remote_copy(
            src_ref=fr_sum, dst_ref=fr_dim.at[k],
            send_sem=g_send.at[k], recv_sem=g_recv.at[k],
            device_id=(r, dim_peers[k]), device_id_type=MESH,
        ).wait_recv()
        total = total + fr_dim[k]
    frac_out[...] = total
    own.wait()
    for copy in a2a:
        copy.wait()


def shards(entity_table, relations, thresholds, head_ids, rel_ids, thr_idx):
    R = lax.axis_size("rows")
    N = lax.axis_size("dim")
    n, width = entity_table.shape
    Q = head_ids.shape[0]
    blocks = Q // lanes
    per = blocks // R
    steps = bits_of(R) + bits_of(N)
    pieces = len(plan_for(N))
    f32 = jnp.float32
    DMA = pltpu.SemaphoreType.DMA
    smem = pl.BlockSpec(memory_space=pltpu.SMEM)
    vmem = pl.BlockSpec(memory_space=pltpu.VMEM)
    hbm = pl.BlockSpec(memory_space=pl.ANY)
    operands = [head_ids, rel_ids, thresholds, thr_idx.reshape(blocks, 1, lanes), relations, entity_table]
    if (width // N) % lanes:
        operands.append(entity_table.reshape(n, N, width // N).transpose(1, 0, 2))
    serving, share = pl.pallas_call(
        functools.partial(kernel, R, N, n * R * N),
        out_shape=(
            jax.ShapeDtypeStruct((n * N, width // N), f32),
            jax.ShapeDtypeStruct((per, 1, lanes), f32),
        ),
        in_specs=[smem, smem, smem, vmem, vmem] + [hbm] * (len(operands) - 5),
        out_specs=(hbm, vmem),
        scratch_shapes=[
            pltpu.VMEM((n, width), f32),
            pltpu.VMEM((n, width), jnp.bfloat16),
            pltpu.VMEM((Q, width), f32),
            pltpu.VMEM((Q, width), f32),
            pltpu.VMEM((Q, width), f32),
            pltpu.VMEM((2 * lanes, width), jnp.bfloat16),
            pltpu.VMEM((blocks, 1, lanes), f32),
            pltpu.VMEM((blocks, 1, lanes), f32),
            pltpu.VMEM((R - 1, per, 1, lanes), f32),
            pltpu.VMEM((N - 1, per, 1, lanes), f32),
            pltpu.VMEM((per, 1, lanes), f32),
            DMA, DMA,
            DMA((pieces, N - 1)), DMA((pieces, N - 1)),
            DMA((2, 2 * steps)), DMA((2, 2 * steps)),
            DMA((R - 1,)), DMA((R - 1,)),
            DMA((N - 1,)), DMA((N - 1,)),
        ],
        compiler_params=pltpu.CompilerParams(
            collective_id=0, has_side_effects=True, vmem_limit_bytes=60 * 2**20
        ),
    )(*operands)
    mine = Q // (R * N)
    fraction = lax.dynamic_slice(share.reshape(Q // R), (lax.axis_index("dim") * mine,), (mine,))
    return serving, fraction


def solution(mesh):
    placed = (P(("rows", "dim"), None), P(), P(), P(), P(), P())
    return jax.shard_map(
        shards,
        mesh=mesh,
        in_specs=placed,
        out_specs=(P("rows", "dim"), P(("rows", "dim"))),
        check_vma=False,
    )
```

time: 401 us -> 210 us (0.52)
  waiting for transfers between devices: 223 us -> 0 us
  Pallas kernels: 0 us -> 202 us
  other arithmetic: 54.6 us -> 0 us
  blocking collectives: 39.4 us -> 0 us
  local copies, waits for them, and re-layouts: 38.8 us -> 7.05 us
  matrix products: 22.6 us -> 0 us
  between operations: 14.2 us -> 0.64 us
  starting transfers between devices: 6.48 us -> 0 us
    psum x1 -> x0, waiting for transfers between devices: 223 us -> none  [shards(): head_vecs = lax.psum(partial_value, ('rows', 'dim'))]
    pallas_call x0 -> x1, Pallas kernels: none -> 202 us  [shards(): pl.pallas_call(functools.partial(kernel, R, N, n * R * N), out_shape=(jax...]
    select_n x2 -> x0, other arithmetic: 43.9 us -> none  [the longest x1 39.9 us: shards(): level = jnp.take(thresholds, thr_idx)]
    unnamed x1 -> x0, blocking collectives: 39.4 us -> none
    gather x6 -> x0, local copies, waits for them, and re-layouts: 24.6 us -> none  [the longest x1 12.9 us: pick_rows(): picked = jnp.take(table, jnp.clip(local, 0, count - 1), axis=0)]
    dot_general x4 -> x0, matrix products: 22.6 us -> none  [score_block(): score = jnp.dot(rows_q, ent_low.T, preferred_element_type=jnp.float32)]
    convert_element_type x2 -> x0, other arithmetic: 10.6 us -> none  [the longest x1 5.89 us: shards(): ent_low = entity_table.astype(jnp.bfloat16)]
    all_to_all x1 -> x0, local copies, waits for them, and re-layouts: 7.44 us -> none  [shards(): lax.all_to_all(entity_table, 'dim', split_axis=1, concat_axis=0, tiled=True)]
  transfers between devices with their start and end apart: 2 -> 0, of which waited for: 1 -> 0; matrix products, arithmetic and copies ran while one was open for 26% -> 0% of each run, Pallas kernels for 0% -> 0%
where the time goes in v1:
time: 210 us
  Pallas kernels  202 us (96%)
  local copies, waits for them, and re-layouts  7.05 us (3%)
    pallas_call x1, Pallas kernels, shards(): pl.pallas_call(functools.partial(kernel, R, N, n * R * N), out_shape=(jax...  202 us
    unnamed x1, local copies, waits for them, and re-layouts  5.85 us

profile of v1, /device:TPU:0, one launch (start us, length us, event | category | flops | bytes accessed | tf_op | source)
XLA Modules:
  0.0 209.6 jit_solution(6439047316747164978)
XLA Ops:
  0.6 201.9 %shard_map.77 = (f32[16384,128]{1,0:T(8,128)}, f32[2,1,128]{2,1,0:T(1,128)}) custom-call(s32[2048]{0:T(1024)} %head_ids.1, s32[2048]{0:T(1024)} %rel_ids.1, f32[64]{0:T(128)} %thr.1, s32[16,1,128]{2,1,0:T(1,128)} %bitcast.2, f32[822,512]{1,0:T(8,128)} %rel.1, f32[4096,512]{1,0:T(8,128)} %table.1), custom_call_target="tpu_custom_call" | custom-call | tf_op jit(solution)/shard_map/pallas_call | solution.py:300
  202.5 1.2 dynamic_slice.3
  203.7 5.9 %copy.9 = f32[16384,128]{1,0:T(8,128)} copy(f32[16384,128]{1,0:T(8,128)} %get-tuple-element.8) | data formatting | bytes 16777216

commit v2 on v1

--- a/solution.py
+++ b/solution.py
@@ -22,6 +22,14 @@
 def bits_of(size):
     assert size & (size - 1) == 0
     return size.bit_length() - 1
+
+
+def flipped(index, mask):
+    out = index
+    for b in range(mask.bit_length()):
+        if (mask >> b) & 1:
+            out = out + (1 - 2 * lax.rem(index // (2 ** b), 2)) * (2 ** b)
+    return out
 
 
 def kernel(
@@ -46,7 +54,7 @@
     load.start()
 
     row_peers = [lax.rem(r + k, R) for k in range(1, R)]
-    dim_peers = [lax.rem(d + k, N) for k in range(1, N)]
+    dim_peers = [flipped(d, k) for k in range(1, N)]
     barrier = pltpu.get_barrier_semaphore()
     for t in row_peers:
         pl.semaphore_signal(barrier, inc=1, device_id=(t, d), device_id_type=MESH)
@@ -260,8 +268,8 @@
     sends = []
     for k, t in enumerate(dim_peers):
         copy = pltpu.make_async_remote_copy(
-            src_ref=fr_sum, dst_ref=fr_dim.at[N - 2 - k],
-            send_sem=g_send.at[k], recv_sem=g_recv.at[N - 2 - k],
+            src_ref=fr_sum, dst_ref=fr_dim.at[k],
+            send_sem=g_send.at[k], recv_sem=g_recv.at[k],
             device_id=(r, t), device_id_type=MESH,
         )
         copy.start()

time: 210 us -> 210 us (level)
  no operation moved by 1% of the time
where the time goes in v2:
time: 210 us
  Pallas kernels  202 us (96%)
  local copies, waits for them, and re-layouts  7.05 us (3%)
    pallas_call x1, Pallas kernels, shards(): pl.pallas_call(functools.partial(kernel, R, N, n * R * N), out_shape=(jax...  202 us
    unnamed x1, local copies, waits for them, and re-layouts  5.85 us

profile of v2, /device:TPU:0, one launch (start us, length us, event | category | flops | bytes accessed | tf_op | source)
XLA Modules:
  0.0 209.7 jit_solution(7002829877555750543)
XLA Ops:
  0.6 202.0 %shard_map.77 = (f32[16384,128]{1,0:T(8,128)}, f32[2,1,128]{2,1,0:T(1,128)}) custom-call(s32[2048]{0:T(1024)} %head_ids.1, s32[2048]{0:T(1024)} %rel_ids.1, f32[64]{0:T(128)} %thr.1, s32[16,1,128]{2,1,0:T(1,128)} %bitcast.2, f32[822,512]{1,0:T(8,128)} %rel.1, f32[4096,512]{1,0:T(8,128)} %table.1), custom_call_target="tpu_custom_call" | custom-call | tf_op jit(solution)/shard_map/pallas_call | solution.py:308
  202.6 1.2 dynamic_slice.3
  203.8 5.9 %copy.9 = f32[16384,128]{1,0:T(8,128)} copy(f32[16384,128]{1,0:T(8,128)} %get-tuple-element.8) | data formatting | bytes 16777216
